TPU v7x, 32 devices: a whole 2x2x4 slice. The times are simulated.
32 devices in a mesh: vocab: 4 (over x, core), expert: 8 (over z, y).
Axes of the slice: x: 2, y: 2, z: 4, core: 2. Of those that a mesh axis runs over, the one named last changes fastest.
Arguments:
- leading_batch_features: bfloat16 [256, 2880], P(('vocab', 'expert')), may hold values from -48 to 48
- sampling_heat_selector: int32 [256], replicated, may hold values from 0 to 3
- output_embedding_matrix: bfloat16 [50272, 2880], P(('vocab', 'expert')), may hold values from -3.354102 to 3.354102
- trailing_batch_features: bfloat16 [512, 2880], P('expert'), may hold values from -6 to 6
- routed_specialist_choice: int32 [512, 4], P('expert'), may hold values from 0 to 31, all different within a row; in each aligned block of 64 rows (0 to 63, 64 to 127, ...) at most 16 rows name the same one
- dispatcher_projection: bfloat16 [2880, 32], replicated, may hold values from -13.416408 to 13.416408
- specialist_gating_matrix: bfloat16 [32, 2880, 1440], P('expert', None, 'vocab'), may hold values from -0.109375 to 0.109375
- specialist_raising_matrix: bfloat16 [32, 2880, 1440], P('expert', None, 'vocab'), may hold values from -0.109375 to 0.109375
- expert_lowering_matrix: bfloat16 [32, 1440, 2880], P('expert', 'vocab'), may hold values from -0.15625 to 0.15625
Outputs:
- lexicon_log_probability: float32 [256, 50272], P(None, ('vocab', 'expert'))
- moe_out: bfloat16 [512, 2880], P('expert', 'vocab')
Inputs may be any that keep to these rules, and one draw needn't show every extreme that they name: `routed_specialist_choice`: in the rows of one index of the expert axis no expert is named more than 16 times, a bound that some block reaches.
All inputs are finite; a program needn't handle non-finite values.
Results may differ from a plain program's by a relative error of at most 0.005.
The roundings to bfloat16 on the way count: a program that leaves them out, or rounds other values in their place, can miss the bound.
Values may be sent and summed in bfloat16 or wider, within the bound.
A program may use at most 256 MiB of HBM per device.

v0:
```python
import functools

import jax
import jax.numpy as jnp
from jax import lax
from jax.experimental import pallas as pl
from jax.experimental.pallas import tpu as pltpu
from jax.sharding import PartitionSpec as P

MESH = pl.DeviceIdType.MESH
ANY = pl.BlockSpec(memory_space=pl.ANY)
VMEM = pl.BlockSpec(memory_space=pltpu.VMEM)


def stats_kernel(nv, ne, mine_ref, out_ref, held, send_sem, recv_sem):
    n = nv * ne
    me = lax.axis_index("vocab") * ne + lax.axis_index("expert")

    def coords(index):
        return (index // ne, lax.rem(index, ne))

    barrier = pltpu.get_barrier_semaphore()

    @pl.loop(1, n)
    def _(i):
        pl.semaphore_signal(
            barrier, inc=1, device_id=coords(lax.rem(me + i, n)), device_id_type=MESH
        )

    pl.semaphore_wait(barrier, n - 1)

    def copy(i, slot):
        return pltpu.make_async_remote_copy(
            src_ref=mine_ref,
            dst_ref=held.at[slot],
            send_sem=send_sem.at[i],
            recv_sem=recv_sem.at[i],
            device_id=coords(lax.rem(me + i, n)),
            device_id_type=MESH,
        )

    @pl.loop(1, n)
    def _(i):
        copy(i, me).start()

    held[pl.ds(me, 1)] = mine_ref[...][None]

    @pl.loop(1, n)
    def _(i):
        copy(i, lax.rem(me + n - i, n)).wait()

    tops = held[:, 0, :]
    top = jnp.max(tops, axis=0, keepdims=True)
    total = jnp.sum(held[:, 1, :] * jnp.exp(tops - top), axis=0, keepdims=True)
    out_ref[0:1, :] = top
    out_ref[1:2, :] = jnp.log(total)


def merge_stats(stats, nv, ne):
    n = nv * ne
    return pl.pallas_call(
        functools.partial(stats_kernel, nv, ne),
        out_shape=jax.ShapeDtypeStruct(stats.shape, jnp.float32),
        in_specs=[VMEM],
        out_specs=VMEM,
        scratch_shapes=[
            pltpu.VMEM((n,) + stats.shape, jnp.float32),
            pltpu.SemaphoreType.DMA((n,)),
            pltpu.SemaphoreType.DMA((n,)),
        ],
        compiler_params=pltpu.CompilerParams(collective_id=0, has_side_effects=True),
        name="merge_stats",
    )(stats)


def moe_kernel(width, x_ref, p_ref, wg_ref, wu_ref, wd_ref, o_ref):
    first = pl.program_id(0) == 0
    x = x_ref[:, :width]
    gate = jnp.dot(x, wg_ref[0], preferred_element_type=jnp.float32)
    up = jnp.dot(x, wu_ref[0], preferred_element_type=jnp.float32)
    act = (gate * jax.nn.sigmoid(1.702 * gate) * (up + 1.0)).astype(jnp.bfloat16)
    prob = p_ref[0]
    span = o_ref.shape[2]
    for v in range(o_ref.shape[0]):
        part = prob * jnp.dot(
            act, wd_ref[0, :, v * span : (v + 1) * span], preferred_element_type=jnp.float32
        )

        @pl.when(first)
        def _():
            o_ref[v] = part

        @pl.when(jnp.logical_not(first))
        def _():
            o_ref[v] += part


def experts(x, probs, wg, wu, wd, nv):
    tokens = x.shape[0]
    local, width, ff = wg.shape
    return pl.pallas_call(
        functools.partial(moe_kernel, width),
        grid=(local,),
        out_shape=jax.ShapeDtypeStruct((nv, tokens, width // nv), jnp.float32),
        in_specs=[
            pl.BlockSpec(x.shape, lambda e: (0, 0)),
            pl.BlockSpec((1, tokens, 1), lambda e: (e, 0, 0)),
            pl.BlockSpec((1, width, ff), lambda e: (e, 0, 0)),
            pl.BlockSpec((1, width, ff), lambda e: (e, 0, 0)),
            pl.BlockSpec((1, ff, width), lambda e: (e, 0, 0)),
        ],
        out_specs=pl.BlockSpec((nv, tokens, width // nv), lambda e: (0, 0, 0)),
        compiler_params=pltpu.CompilerParams(vmem_limit_bytes=60 * 1024 * 1024),
        cost_estimate=pl.CostEstimate(
            flops=6 * local * tokens * width * ff,
            bytes_accessed=6 * local * width * ff,
            transcendentals=0,
        ),
        name="experts",
    )(x, probs, wg, wu, wd)


def per_device(nv, ne, lead, heat, embed, tok, choice, router, wg, wu, wd):
    width = tok.shape[1]
    top_count = choice.shape[1]
    local = wg.shape[0]
    rows = tok.shape[0]
    quarter = rows // nv
    v = lax.axis_index("vocab")
    pad = (-width) % 128
    pad = pad if pad >= top_count else pad + 128
    packed = jnp.concatenate(
        [
            tok,
            choice.astype(jnp.bfloat16),
            jnp.zeros((rows, pad - top_count), jnp.bfloat16),
        ],
        axis=1,
    )
    mine = lax.dynamic_slice_in_dim(packed, v * quarter, quarter, axis=0)
    x = lax.all_gather(mine, ("expert", "vocab"), axis=0, tiled=True)
    lead_all = lax.all_gather(lead, ("vocab", "expert"), axis=0, tiled=True)

    ids = x[:, width : width + top_count].astype(jnp.int32)
    router_full = jnp.dot(x[:, :width], router, preferred_element_type=jnp.float32)
    hot = ids[:, :, None] == jnp.arange(router.shape[1], dtype=jnp.int32)[None, None, :]
    scores = jnp.sum(jnp.where(hot, router_full[:, None, :], 0.0), axis=2)
    gate_probs = jax.nn.softmax(scores, axis=1)
    base = lax.axis_index("expert") * local
    here = ids[None, :, :] == (base + jnp.arange(local, dtype=jnp.int32))[:, None, None]
    probs = jnp.sum(jnp.where(here, gate_probs[None], 0.0), axis=2)[:, :, None]
    part = experts(x, probs, wg, wu, wd, nv)
    part = part.reshape(nv * ne, rows, width // nv)
    moe = lax.psum_scatter(part, ("vocab", "expert"), scatter_dimension=0, tiled=True)
    moe = moe[0].astype(jnp.bfloat16)

    temp = 0.5 + 0.25 * heat.astype(jnp.float32)
    scaled = (
        lax.dot_general(
            lead_all, embed, (((1,), (1,)), ((), ())), preferred_element_type=jnp.float32
        )
        / temp[:, None]
    )
    top = jnp.max(scaled, axis=1)
    total = jnp.sum(jnp.exp(scaled - top[:, None]), axis=1)
    merged = merge_stats(jnp.stack([top, total]), nv, ne)
    logp = scaled - merged[0][:, None] - merged[1][:, None]
    return logp, moe


def solution(mesh):
    nv, ne = mesh.shape["vocab"], mesh.shape["expert"]
    placed = (
        P(("vocab", "expert"), None),
        P(),
        P(("vocab", "expert"), None),
        P("expert", None),
        P("expert", None),
        P(),
        P("expert", None, "vocab"),
        P("expert", None, "vocab"),
        P("expert", "vocab", None),
    )
    return jax.shard_map(
        functools.partial(per_device, nv, ne),
        mesh=mesh,
        in_specs=placed,
        out_specs=(P(None, ("vocab", "expert")), P("expert", "vocab")),
        check_vma=False,
    )
```

profile of v0, /device:TPU:0, one launch (start us, length us, event | category | flops | bytes accessed | tf_op | source)
XLA Modules:
  0.0 257.3 jit_solution(16705140760048152429)
XLA Ops:
  7.2 0.0 copy-start
  7.2 0.0 all-gather.5.cloned.1.call-start
  7.2 0.7 convert_element_type.16
  8.0 0.1 copy.26
  8.1 1.1 concatenate.3
  9.2 0.7 constant_dynamic-slice_fusion
  9.8 0.0 all-gather.5.cloned.1.call-update
  9.8 0.0 all-gather.3.cloned.1.call-start
  9.9 0.7 all-gather.3.cloned.1.call-update
  10.6 0.0 reduce-scatter.2.cloned.1.call-start
  10.6 11.6 %copy.30.wg_ref = bf16[4,2880,360]{2,1,0:T(8,128)(2,1)} copy(bf16[4,2880,360]{1,2,0:T(8,128)(2,1)} %param.15) | data formatting | bytes 16588800 | tf_op args[6]
  22.3 11.6 %copy.31.wu_ref = bf16[4,2880,360]{2,1,0:T(8,128)(2,1)} copy(bf16[4,2880,360]{1,2,0:T(8,128)(2,1)} %param.16) | data formatting | bytes 16588800 | tf_op args[7]
  33.9 39.1 %all-gather.5.cloned.1.call-done.x_ref = bf16[512,2944]{1,0:T(8,128)(2,1)} async-done(((bf16[16,2944]{1,0:T(8,128)(2,1)}), bf16[512,2944]{1,0:T(8,128)(2,1)}) %all-gather.5.cloned.1.call-update) | async-done | bytes 3014672 | tf_op jit(solution)/shard_map/all_gather | solution.py:141
  73.0 1.0 slice_convert_fusion
  74.0 0.1 copy.27
  74.1 0.0 copy-done
  74.1 2.8 %fusion = f32[512,32]{0,1:T(8,128)S(1)} fusion(bf16[2880,32]{0,1:T(8,128)(2,1)S(1)} %copy-done, bf16[512,2944]{1,0:T(8,128)(2,1)} %all-gather.5.cloned.1.call-done.x_ref), kind=kOutput, calls=%fused_computation | convolution fusion | flops 94371840 | bytes 3264512 | tf_op jit(solution)/shard_map/dot_general | solution.py:145
  76.9 0.1 select_reduce_fusion
  77.1 0.1 select_reduce_fusion.1
  77.2 1.3 copy.29.p_ref
  78.5 34.4 %experts.1 = f32[4,512,720]{2,1,0:T(8,128)} custom-call(bf16[512,2944]{1,0:T(8,128)(2,1)} %all-gather.5.cloned.1.call-done.x_ref, f32[4,512,1]{2,1,0:T(8,128)} %copy.29.p_ref, bf16[4,2880,360]{2,1,0:T(8,128)(2,1)} %copy.30.wg_ref, bf16[4,2880,360]{2,1,0:T(8,128)(2,1)} %copy.31.wu_ref, bf16[4,360,2880]{2,1,0:T(8,128)(2,1)} %wd_ref.1), custom_call_target="tpu_custom_call" | custom-call | flops 12740198400 | bytes 24883200 | tf_op jit(solution)/shard_map/experts/pallas_call | solution.py:101
  112.9 0.0 copy-start.2
  112.9 0.0 reduce-scatter.2.cloned.1.call-update
  112.9 0.7 copy-done.2
  113.6 16.0 %all-gather.3.cloned.1.call-done = bf16[256,2880]{1,0:T(8,128)(2,1)} async-done(((bf16[8,2880]{1,0:T(8,128)(2,1)}), bf16[256,2880]{1,0:T(8,128)(2,1)}) %all-gather.3.cloned.1.call-update) | async-done | bytes 1474576 | tf_op jit(solution)/shard_map/all_gather | solution.py:142
  129.6 5.8 %fusion.5 = (f32[256]{0:T(256)S(1)}, f32[256,1571]{0,1:T(8,128)S(1)}) fusion(f32[256]{0:T(256)S(1)} %multiply_add_fusion, bf16[256,2880]{1,0:T(8,128)(2,1)} %all-gather.3.cloned.1.call-done, bf16[1571,2880]{1,0:T(8,128)(2,1)} %param.11), kind=kOutput, calls=%fused_computation.18 | convolution fusion | flops 2317337856 | bytes 12134272 | tf_op jit(solution)/shard_map/dot_general | solution.py:159
  135.4 0.3 exponential_reduce_fusion
  135.7 0.6 pad_maximum_fusion.mine_ref
  136.3 9.7 %merge_stats.1 = f32[2,256]{1,0:T(2,128)} custom-call(f32[2,256]{1,0:T(2,128)} %pad_maximum_fusion.mine_ref), custom_call_target="tpu_custom_call" | custom-call | tf_op jit(solution)/shard_map/merge_stats/pallas_call | solution.py:61
  146.0 0.8 fusion.4
  146.8 0.0 copy-start.1
  146.8 1.3 subtract_subtract_fusion
  148.0 101.1 %reduce-scatter.2.cloned.1.call-done = f32[1,64,720]{2,1,0:T(8,128)} async-done(((f32[32,64,720]{2,1,0:T(8,128)}), f32[1,64,720]{2,1,0:T(8,128)}) %reduce-scatter.2.cloned.1.call-update) | async-done | bytes 184336 | tf_op jit(solution)/shard_map/reduce_scatter | solution.py:154
  249.2 1.6 convert_bitcast_fusion
  250.7 0.0 copy-done.1
  (6 shorter events, 0.1 us)
Async XLA Ops:
  7.2 66.9 %copy-start = (bf16[2880,32]{0,1:T(8,128)(2,1)S(1)}, bf16[2880,32]{0,1:T(8,128)(2,1)}, u32[]{:S(2)}) copy-start(bf16[2880,32]{0,1:T(8,128)(2,1)} %param.14) | copy-start | bytes 552964
  7.2 65.8 %all-gather.5.cloned.1.call-start = ((), (), s32[]{:S(2)}) async-start(), calls=%async_computation.2 | async-start | bytes 3108864 | tf_op jit(solution)/shard_map/all_gather | solution.py:141
  9.8 119.7 %all-gather.3.cloned.1.call-start = ((), (), s32[]{:S(2)}) async-start(), calls=%async_computation.1 | async-start | bytes 1554432 | tf_op jit(solution)/shard_map/all_gather | solution.py:142
  10.6 238.6 %reduce-scatter.2.cloned.1.call-start = ((), (), s32[]{:S(2)}) async-start(), calls=%async_computation.3 | async-start | bytes 6488064 | tf_op jit(solution)/shard_map/reduce_scatter | solution.py:154
  112.9 0.7 copy-start.2
  146.8 104.0 %copy-start.1 = (bf16[2880,32]{0,1:T(8,128)(2,1)S(1)}, bf16[2880,32]{0,1:T(8,128)(2,1)}, u32[]{:S(2)}) copy-start(bf16[2880,32]{0,1:T(8,128)(2,1)} %param.14) | copy-start | bytes 552964
Sparse Core Ops, SparseCore 0:
  11.4 61.5 all-gather.4
  75.8 53.7 all-gather.2
  135.2 113.9 reduce-scatter.1
where the time goes:
time: 258 us; the launch traced here: 257 us
  waiting for transfers between devices  157 us (61%)
  Pallas kernels  44.1 us (17%)
  local copies, waits for them, and re-layouts  28 us (11%)
  between operations  13.8 us (5%)
  matrix products  8.67 us (3%)
  other arithmetic  5.72 us (2%)
    reduce_scatter x1, waiting for transfers between devices, per_device(): lax.psum_scatter(part, ('vocab', 'expert'), scatter_dimension=0, tiled=True)  101 us
    all_gather x1, waiting for transfers between devices, per_device(): x = lax.all_gather(mine, ('expert', 'vocab'), axis=0, tiled=True)  39.1 us
    pallas_call x1, Pallas kernels, experts(): pl.pallas_call(functools.partial(moe_kernel, width), grid=(local,), out_s...  34.4 us
    unnamed x8, local copies, waits for them, and re-layouts  23.9 us
    all_gather x1, waiting for transfers between devices, per_device(): lead_all = lax.all_gather(lead, ('vocab', 'expert'), axis=0, tiled=True)  16 us
    pallas_call x1, Pallas kernels, merge_stats(): pl.pallas_call(functools.partial(stats_kernel, nv, ne), out_shape=jax.Sha...  9.68 us
    dot_general x1, matrix products, per_device(): lax.dot_general(lead_all, embed, (((1,), (1,)), ((), ())), preferred_elem...  5.84 us
  transfers between devices with their start and end apart: 3, of which 3 were waited for; matrix products, arithmetic and copies ran while one was open for 15% of the time, Pallas kernels for 17%

commit v1 on v0

v1 whole, which is shorter than its diff:
```python
import functools

import jax
import jax.numpy as jnp
from jax import lax
from jax.experimental import pallas as pl
from jax.experimental.pallas import tpu as pltpu
from jax.sharding import PartitionSpec as P

MESH = pl.DeviceIdType.MESH
ANY = pl.BlockSpec(memory_space=pl.ANY)
VMEM = pl.BlockSpec(memory_space=pltpu.VMEM)
CORES = 2
UNIT = 8
F32 = jnp.float32
BF16 = jnp.bfloat16


def dot_nt(a, b):
    return lax.dot_general(a, b, (((1,), (1,)), ((), ())), preferred_element_type=F32)


def body(
    dims,
    lead_ref, heat_ref, embed_ref, tok_ref, choice_ref, router_ref, wg_ref, wu_ref, wd_ref,
    sc_ref, norm_ref, moe_ref,
    embed_v, wg_v, wu_v, wd_raw, wd_v, xblk, lead_v, heat_v, choice_v, router_v, ptile, held, x2, pcol,
    act, logits, s_send, s_own, s_recv, sb3, rb3, sb2, rb2, sbz, rbz, acc, stat_mine, stat_all,
    sem_small, sem_l, sem_w, sem_raw, gs, gr, sem_ss, sem_sr, s3s, s3r, s2s, s2r, szs, szr, st_s, st_r,
):
    nv, ne, nx, na, nb = dims
    n = nv * ne
    v = lax.axis_index("vocab")
    e = lax.axis_index("expert")
    x, c = v // CORES, lax.rem(v, CORES)
    a, b = e // nb, lax.rem(e, nb)
    n1, n2, n3 = na, nb, nx
    if nx == nb:
        p2 = jnp.where(c == 0, b, x)
        p3 = jnp.where(c == 0, x, b)
    else:
        p2, p3 = b, x

    def dev(a_, p2_, p3_, c_):
        if nx == nb:
            b_ = jnp.where(c == 0, p2_, p3_)
            x_ = jnp.where(c == 0, p3_, p2_)
        else:
            b_, x_ = p2_, p3_
        return (x_ * CORES + c_, a_ * nb + b_)

    def wrap(i, size):
        return jnp.where(i >= size, i - size, i)

    groups = held.shape[0]
    nq = groups - 1

    def near(da, d2, d3):
        return wrap(a + da, n1), wrap(p2 + d2, n2), wrap(p3 + d3, n3)

    def others(act_on):
        for dv in range(nv):

            @pl.loop(0 if dv else 1, ne)
            def _(de):
                act_on(wrap(v + dv, nv), wrap(e + de, ne), dv * ne + de)

    def slot(g, a_, p2_, p3_, c_):
        v_, e_ = dev(a_, p2_, p3_, c_)
        return v_ * ne + e_ if g == nq else e_ * nv + v_

    me = e * nv + v
    width = xblk.shape[2]
    nexp = router_v.shape[0]
    local, ff, _ = wg_v.shape
    raw_depth = wd_raw.shape[0]
    span = wd_v.shape[3]
    rows = xblk.shape[0] * UNIT

    small = [
        pltpu.make_async_copy(tok_ref, xblk, sem_small.at[0]),
        pltpu.make_async_copy(choice_ref, choice_v, sem_small.at[1]),
        pltpu.make_async_copy(router_ref, router_v, sem_small.at[2]),
        pltpu.make_async_copy(heat_ref, heat_v, sem_small.at[3]),
        pltpu.make_async_copy(lead_ref, lead_v, sem_small.at[4]),
    ]
    raw = [pltpu.make_async_copy(wd_ref.at[l], wd_raw.at[l % raw_depth], sem_raw.at[l]) for l in range(local)]
    wg_in = [pltpu.make_async_copy(wg_ref.at[l], wg_v.at[l], sem_w.at[0, l]) for l in range(local)]
    wu_in = [pltpu.make_async_copy(wu_ref.at[l], wu_v.at[l], sem_w.at[1, l]) for l in range(local)]
    depth, tile = logits.shape[0], logits.shape[1]
    vocab = embed_ref.shape[0]
    tiles = -(-vocab // tile)

    def extent(t):
        return t * tile, min(tile, vocab - t * tile)

    def sc_out(t):
        at = t * tile
        return pltpu.make_async_copy(
            logits.at[t % depth], sc_ref.at[at : at + tile], sem_l.at[t]
        )

    embed_in = pltpu.make_async_copy(embed_ref, embed_v, sem_small.at[5])

    for copy in small:
        copy.start()

    barrier = pltpu.get_barrier_semaphore()

    def greet(v_, e_, k):
        pl.semaphore_signal(barrier, inc=1, device_id=(v_, e_), device_id_type=MESH)

    others(greet)

    for l in range(min(raw_depth, local)):
        raw[l].start()
    for l in range(local):
        wg_in[l].start()
        wu_in[l].start()
    embed_in.start()

    for copy in small:
        copy.wait()
    scores = dot_nt(router_v[...], xblk[...].reshape(rows, width))
    ids = choice_v[...]
    expert = lax.broadcasted_iota(jnp.int32, (nexp, rows), 0)
    hot = expert == ids[0:1, :]
    for k in range(1, ids.shape[0]):
        hot = jnp.logical_or(hot, expert == ids[k : k + 1, :])
    peak = jnp.max(jnp.where(hot, scores, -jnp.inf), axis=0, keepdims=True)
    weight = jnp.where(hot, jnp.exp(jnp.where(hot, scores - peak, 0.0)), 0.0)
    prob = weight / jnp.sum(weight, axis=0, keepdims=True)
    high = prob.astype(BF16).astype(F32)
    ptile[...] = jnp.zeros_like(ptile)
    ptile[0:nexp, 0:rows] = high
    ptile[nexp : 2 * nexp, 0:rows] = prob - high
    ptile[...] = ptile[...].T
    for q in range(nq):
        unit = v * nq + q
        held[q, me, :, 0:width] = xblk[unit]
        start = pl.multiple_of(unit * UNIT, UNIT)
        held[q, me, :, width : width + 2 * nexp] = ptile[pl.ds(start, UNIT), 0 : 2 * nexp].astype(
            BF16
        )

    held[nq, v * ne + e, :, 0:width] = lead_v[...]

    pl.semaphore_wait(barrier, n - 1)

    base2 = n1 - 1
    base3 = base2 + (n2 - 1) * n1
    base_s = base3 + (n3 - 1) * n1 * n2

    def gcopy(g, s, k, target):
        return pltpu.make_async_remote_copy(
            src_ref=held.at[g, s],
            dst_ref=held.at[g, s],
            send_sem=gs.at[g, k],
            recv_sem=gr.at[g, s],
            device_id=target,
            device_id_type=MESH,
        )

    def forward(g, da, d2, d3, stage):
        s = slot(g, *near(da, d2, d3), c)
        if stage <= 1:
            for k2 in range(1, n2):
                gcopy(g, s, base2 + (k2 - 1) * n1 + da, dev(*near(0, k2, 0), c)).start()
        if stage <= 2:
            for k3 in range(1, n3):
                gcopy(g, s, base3 + ((k3 - 1) * n2 + d2) * n1 + da, dev(*near(0, 0, k3), c)).start()
        gcopy(g, s, base_s + (d3 * n2 + d2) * n1 + da, dev(a, p2, p3, 1 - c)).start()

    def arrive(g, s):
        gcopy(g, s, 0, dev(a, p2, p3, 1 - c)).wait_recv()

    def g_start(g):
        for d in range(1, n1):
            gcopy(g, slot(g, *near(0, 0, 0), c), d - 1, dev(*near(d, 0, 0), c)).start()
        forward(g, 0, 0, 0, 1)

    def g_one(g):
        @pl.loop(1, n1)
        def _(da):
            arrive(g, slot(g, *near(da, 0, 0), c))
            forward(g, da, 0, 0, 1)

    def g_two(g):
        for d2 in range(1, n2):

            @pl.loop(0, n1)
            def _(da):
                arrive(g, slot(g, *near(da, d2, 0), c))
                forward(g, da, d2, 0, 2)

    def g_three(g, d2s=None):
        for d2 in range(n2) if d2s is None else d2s:
            for d3 in range(1, n3):

                @pl.loop(0, n1)
                def _(da):
                    arrive(g, slot(g, *near(da, d2, d3), c))
                    forward(g, da, d2, d3, 3)

    def g_sib(g):
        for d3 in range(n3):
            for d2 in range(n2):

                @pl.loop(0, n1)
                def _(da):
                    arrive(g, slot(g, *near(da, d2, d3), 1 - c))

    def g_end(g):
        @pl.loop(0, n - 1)
        def _(k):
            gcopy(g, me, k, dev(a, p2, p3, 1 - c)).wait_send()

    def wd_shift(l):
        raw[l].wait()
        for w in range(nv):
            wd_v[l, w] = wd_raw[l % raw_depth, :, w * span : (w + 1) * span]
        if l + raw_depth < local:
            raw[l + raw_depth].start()

    def load_x(g):
        x2[...] = held[g, :, :, 0:width].reshape(n * UNIT, width)

    def load_p(q):
        tail = held[q, :, :, width : width + 2 * nexp].reshape(n * UNIT, 2 * nexp).astype(F32)
        lane = lax.rem(lax.broadcasted_iota(jnp.int32, tail.shape, 1), nexp)
        for l in range(local):
            pcol[:, l : l + 1] = jnp.sum(
                jnp.where(lane == e * local + l, tail, 0.0), axis=1, keepdims=True
            )

    def gate_up(l):
        gate = dot_nt(wg_v[l], x2[...])
        up = dot_nt(wu_v[l], x2[...])
        act[l] = (gate * jax.nn.sigmoid(1.702 * gate) * (up + 1.0)).astype(BF16).T

    def down(w):
        total = pcol[:, 0:1] * jnp.dot(act[0], wd_v[0, w], preferred_element_type=F32)
        for l in range(1, local):
            total += pcol[:, l : l + 1] * jnp.dot(act[l], wd_v[l, w], preferred_element_type=F32)
        return total.reshape(ne, n * UNIT // ne, span)

    def scopy(q, j):
        return pltpu.make_async_remote_copy(
            src_ref=s_send.at[q, j],
            dst_ref=s_recv.at[q, j],
            send_sem=sem_ss.at[q, j],
            recv_sem=sem_sr.at[q, j],
            device_id=dev(a, p2, p3, 1 - c),
            device_id_type=MESH,
        )

    def down_send(q):
        @pl.loop(0, nx)
        def _(j):
            s_send[q, j] = down(j * CORES + 1 - c).astype(s_send.dtype)
            scopy(q, j).start()

    def down_own(q):
        @pl.loop(0, nx)
        def _(j):
            s_own[q, j] = down(j * CORES + c).astype(s_own.dtype)

    def chip(q, a_, p2_, p3_):
        v_, e_ = dev(a_, p2_, p3_, c)
        x_ = v_ // CORES
        return s_own[q, x_, e_].astype(F32) + s_recv[q, x_, e_].astype(F32)

    shared = len(sb3.shape) == 2
    sb3 = s_send if shared else sb3

    def c3(q, d3, i, target):
        return pltpu.make_async_remote_copy(
            src_ref=sb3.at[q, d3 - 1, i],
            dst_ref=rb3.at[q, d3 - 1, i],
            send_sem=s3s.at[q, d3 - 1, i],
            recv_sem=s3r.at[q, d3 - 1, i],
            device_id=target,
            device_id_type=MESH,
        )

    def c2(q, d2, i, target):
        return pltpu.make_async_remote_copy(
            src_ref=sb2.at[q, d2 - 1, i],
            dst_ref=rb2.at[q, d2 - 1, i],
            send_sem=s2s.at[q, d2 - 1, i],
            recv_sem=s2r.at[q, d2 - 1, i],
            device_id=target,
            device_id_type=MESH,
        )

    def c1(q, d, target):
        return pltpu.make_async_remote_copy(
            src_ref=sbz.at[q, d - 1],
            dst_ref=rbz.at[q, d - 1],
            send_sem=szs.at[q, d - 1],
            recv_sem=szr.at[q, d - 1],
            device_id=target,
            device_id_type=MESH,
        )

    def c_send(q):
        @pl.loop(0, nx)
        def _(j):
            scopy(q, j).wait_recv()
            if shared:
                scopy(q, j).wait_send()

        for d3 in range(1, n3):

            for d2 in range(n2 - 1, -1, -1):

                @pl.loop(0, n1)
                def _(i):
                    a_, p2_, p3_ = near(wrap(i + 1, n1), d2, d3)
                    k = a_ * n2 + p2_
                    sb3[q, d3 - 1, k] = chip(q, a_, p2_, p3_).astype(BF16)
                    c3(q, d3, k, dev(*near(0, 0, d3), c)).start()

    def c_three(q):
        def total(da, d2):
            a_, p2_, p3_ = near(da, d2, 0)
            k = a_ * n2 + p2_
            part = chip(q, a_, p2_, p3_)
            for d3 in range(1, n3):
                c3(q, d3, k, dev(a, p2, p3, 1 - c)).wait_recv()
                part += rb3[q, d3 - 1, k].astype(F32)
            return a_, part

        for d2 in range(n2 - 1, 0, -1):

            @pl.loop(0, n1)
            def _(i):
                a_, part = total(wrap(i + 1, n1), d2)
                sb2[q, d2 - 1, a_] = part.astype(BF16)
                c2(q, d2, a_, dev(*near(0, d2, 0), c)).start()

        @pl.loop(0, n1)
        def _(i):
            a_, part = total(wrap(i + 1, n1), 0)
            acc[q, a_] = part

    def c_two(q):
        def total(a_):
            part = acc[q, a_]
            for d2 in range(1, n2):
                c2(q, d2, a_, dev(a, p2, p3, 1 - c)).wait_recv()
                part += rb2[q, d2 - 1, a_].astype(F32)
            return part

        @pl.loop(1, n1)
        def _(da):
            a_, p2_, p3_ = near(da, 0, 0)
            sbz[q, da - 1] = total(a_).astype(BF16)
            c1(q, da, dev(a_, p2_, p3_, c)).start()

        acc[q, a] = total(a)

    def c_one(q):
        part = acc[q, a]
        for d in range(1, n1):
            c1(q, d, dev(a, p2, p3, 1 - c)).wait_recv()
            part += rbz[q, d - 1].astype(F32)
        part = part.astype(BF16)
        for w in range(nv):
            at = (w * nq + q) * UNIT
            moe_ref[at : at + UNIT, :] = part[w * UNIT : (w + 1) * UNIT]

    def c_end(q):
        nobody = dev(a, p2, p3, 1 - c)

        if not shared:

            @pl.loop(0, nx)
            def _(j):
                scopy(q, j).wait_send()

        for d3 in range(1, n3):

            @pl.loop(0, n1 * n2)
            def _(i):
                c3(q, d3, i, nobody).wait_send()

        for d2 in range(1, n2):

            @pl.loop(0, n1)
            def _(i):
                c2(q, d2, i, nobody).wait_send()

        for d in range(1, n1):
            c1(q, d, nobody).wait_send()

    def lm_tile(t, top, total):
        at, size = extent(t)
        if t == 0:
            embed_in.wait()
        scale = 1.0 / (0.5 + 0.25 * heat_v[...].astype(F32))
        part = dot_nt(embed_v[at : at + size], x2[...]) * scale
        if t >= depth:
            sc_out(t - depth).wait()
        logits[t % depth, 0:size] = part
        sc_out(t).start()
        peak = jnp.maximum(top, jnp.max(part, axis=0, keepdims=True))
        total = total * jnp.exp(top - peak) + jnp.sum(jnp.exp(part - peak), axis=0, keepdims=True)
        return peak, total

    def stat(v_, e_, s, k):
        return pltpu.make_async_remote_copy(
            src_ref=stat_mine,
            dst_ref=stat_all.at[s],
            send_sem=st_s.at[k],
            recv_sem=st_r.at[s],
            device_id=(v_, e_),
            device_id_type=MESH,
        )

    def lm_send(top, total):
        stat_mine[0:1, :] = top
        stat_mine[1:2, :] = total
        stat_all[pl.ds(me, 1)] = stat_mine[...][None]
        others(lambda v_, e_, k: stat(v_, e_, me, k).start())

    def lm_end():
        others(lambda v_, e_, k: stat(v_, e_, e_ * nv + v_, k).wait())
        tops = stat_all[:, 0, :]
        top = jnp.max(tops, axis=0, keepdims=True)
        total = jnp.sum(stat_all[:, 1, :] * jnp.exp(tops - top), axis=0, keepdims=True)
        norm_ref[...] = top + jnp.log(total)
        for t in range(max(0, tiles - depth), tiles):
            sc_out(t).wait()

    last = nq
    for g in range(groups):
        g_start(g)
    g_one(0)
    wd_shift(0)
    g_two(0)
    if nq > 1:
        g_one(1)
    wd_shift(1)
    g_three(0)
    if nq > 1:
        g_two(1)
    g_one(last)
    g_sib(0)
    load_x(0)
    load_p(0)

    def during(q):
        steps = []
        if q + 1 < nq:
            steps += [lambda: g_three(q + 1, [0]), lambda: g_three(q + 1, range(1, n2))]
            if q + 2 < nq:
                steps += [lambda: g_one(q + 2), lambda: g_two(q + 2)]
        if q == 0:
            steps += [lambda: g_two(last)]
            steps += [lambda: g_three(last, [0]), lambda: g_three(last, range(1, n2))]
        if q:
            steps += [lambda: c_send(q - 1), lambda: c_three(q - 1)]
            steps += [lambda: c_two(q - 1), lambda: c_one(q - 1)]
        return steps

    for q in range(nq):
        if q:
            g_sib(q)
            load_x(q)
            load_p(q)
        steps = during(q)
        work = []
        for l in range(local):
            work.append(functools.partial(gate_up, l))
        work += [lambda: down_send(q), lambda: down_own(q)]
        for l, step in enumerate(work):
            if q == 0 and l < local:
                wg_in[l].wait()
                wu_in[l].wait()
                if l >= 2:
                    wd_shift(l)
            step()
            if steps:
                steps.pop(0)()
        for step in steps:
            step()
    q = nq - 1
    g_sib(last)
    load_x(last)
    steps = [lambda: c_send(q), lambda: c_three(q), lambda: c_two(q)]
    top, total = jnp.full((1, n * UNIT), -jnp.inf, F32), jnp.zeros((1, n * UNIT), F32)
    for t in range(tiles):
        if steps:
            steps.pop(0)()
        top, total = lm_tile(t, top, total)
    lm_send(top, total)
    for step in steps:
        step()
    c_one(q)
    lm_end()
    for g in range(groups):
        g_end(g)
    for q in range(nq):
        c_end(q)


def fused(dims, lead, heat, embed, tok, choice, router, wg, wu, wd):
    nv, ne, nx, na, nb = dims
    n = nv * ne
    local, ff, width = wg.shape
    vocab = embed.shape[0]
    rows = tok.shape[0] * UNIT
    nexp = router.shape[0]
    span = width // nv
    nq = tok.shape[0] // nv
    groups = nq + 1
    tokens = n * UNIT
    wide = -(-(width + 2 * nexp) // 128) * 128
    per = tokens // ne
    side = -(-max(2 * nexp, rows) // 128) * 128
    n1, n2, n3 = na, nb, nx
    roomy = 3 * nx * nq * tokens * (-(-span // 128) * 128) * 4 < 10 << 20
    tile = -(-vocab // (64 if roomy else 128)) * 16
    tiles = -(-vocab // tile)
    link, depth = (F32, tiles) if roomy else (BF16, 2)
    dma = pltpu.SemaphoreType.DMA
    scratch = [
        pltpu.VMEM((vocab, width), BF16),
        pltpu.VMEM((local, ff, width), BF16),
        pltpu.VMEM((local, ff, width), BF16),
        pltpu.VMEM((2 if roomy else 1, ff, width), BF16),
        pltpu.VMEM((local, nv, ff, span), BF16),
        pltpu.VMEM(tok.shape, BF16),
        pltpu.VMEM(lead.shape, BF16),
        pltpu.VMEM(heat.shape, jnp.int32),
        pltpu.VMEM(choice.shape, jnp.int32),
        pltpu.VMEM(router.shape, BF16),
        pltpu.VMEM((side, side), F32),
        pltpu.VMEM((groups, n, UNIT, wide), BF16),
        pltpu.VMEM((tokens, width), BF16),
        pltpu.VMEM((tokens, 128), F32),
        pltpu.VMEM((local, tokens, ff), BF16),
        pltpu.VMEM((depth, tile, tokens), F32),
        pltpu.VMEM((nq, nx, ne, per, span), link),
        pltpu.VMEM((nq, nx, ne, per, span), link),
        pltpu.VMEM((nq, nx, ne, per, span), link),
        pltpu.VMEM((nq, n3 - 1, n1 * n2, per, span) if roomy else (8, 128), BF16),
        pltpu.VMEM((nq, n3 - 1, n1 * n2, per, span), BF16),
        pltpu.VMEM((nq, n2 - 1, n1, per, span), BF16),
        pltpu.VMEM((nq, n2 - 1, n1, per, span), BF16),
        pltpu.VMEM((nq, n1 - 1, per, span), BF16),
        pltpu.VMEM((nq, n1 - 1, per, span), BF16),
        pltpu.VMEM((nq, n1, per, span), F32),
        pltpu.VMEM((2, tokens), F32),
        pltpu.VMEM((n, 2, tokens), F32),
        dma((6,)),
        dma((tiles,)),
        dma((2, local)),
        dma((local,)),
        dma((groups, n - 1)),
        dma((groups, n)),
        dma((nq, nx)),
        dma((nq, nx)),
        dma((nq, n3 - 1, n1 * n2)),
        dma((nq, n3 - 1, n1 * n2)),
        dma((nq, n2 - 1, n1)),
        dma((nq, n2 - 1, n1)),
        dma((nq, n1 - 1)),
        dma((nq, n1 - 1)),
        dma((n,)),
        dma((n,)),
    ]
    return pl.pallas_call(
        functools.partial(body, dims),
        out_shape=(
            jax.ShapeDtypeStruct((tiles * tile, tokens), F32),
            jax.ShapeDtypeStruct((1, tokens), F32),
            jax.ShapeDtypeStruct((rows, span), BF16),
        ),
        in_specs=[ANY] * 9,
        out_specs=(ANY, VMEM, VMEM),
        scratch_shapes=scratch,
        compiler_params=pltpu.CompilerParams(
            collective_id=0, has_side_effects=True, vmem_limit_bytes=67043328
        ),
        name="fused",
    )(lead, heat, embed, tok, choice, router, wg, wu, wd)


def per_device(dims, lead, heat, embed, tok, choice, router, wg, wu, wd):
    scaled, norm, moe = fused(
        dims,
        lead,
        heat[None, :],
        embed,
        tok.reshape(tok.shape[0] // UNIT, UNIT, tok.shape[1]),
        choice.T,
        router.T,
        wg.swapaxes(1, 2),
        wu.swapaxes(1, 2),
        wd,
    )
    return (scaled[: embed.shape[0]] - norm).T, moe


def fast_steps(mesh, axis):
    index = mesh.axis_names.index(axis)
    devices = mesh.devices.swapaxes(0, index)[:, 0]
    places = [tuple(d.coords) for d in devices]
    moved = [i for i, (p, q) in enumerate(zip(places[0], places[1])) if p != q]
    count = 1
    while count < len(places):
        if any(p != q and i not in moved for i, (p, q) in enumerate(zip(places[0], places[count]))):
            break
        count += 1
    return count


def solution(mesh):
    nv, ne = mesh.shape["vocab"], mesh.shape["expert"]
    nb = fast_steps(mesh, "expert")
    dims = (nv, ne, nv // CORES, ne // nb, nb)
    placed = (
        P(("vocab", "expert"), None),
        P(),
        P(("vocab", "expert"), None),
        P("expert", None),
        P("expert", None),
        P(),
        P("expert", None, "vocab"),
        P("expert", None, "vocab"),
        P("expert", "vocab", None),
    )
    return jax.shard_map(
        functools.partial(per_device, dims),
        mesh=mesh,
        in_specs=placed,
        out_specs=(P(None, ("vocab", "expert")), P("expert", "vocab")),
        check_vma=False,
    )
```

time: 258 us -> 84.8 us (0.33)
  waiting for transfers between devices: 157 us -> 0 us
  Pallas kernels: 44.1 us -> 80.6 us
  local copies, waits for them, and re-layouts: 28 us -> 0.64 us
  between operations: 13.8 us -> 0.65 us
  matrix products: 8.67 us -> 0 us
  other arithmetic: 5.72 us -> 2.72 us
    reduce_scatter x1 -> x0, waiting for transfers between devices: 101 us -> none  [per_device(): lax.psum_scatter(part, ('vocab', 'expert'), scatter_dimension=0, tiled=True)]
    all_gather x2 -> x0, waiting for transfers between devices: 55.1 us -> none  [the longest x1 39.1 us: per_device(): x = lax.all_gather(mine, ('expert', 'vocab'), axis=0, tiled=True)]
    pallas_call x2 -> x1, Pallas kernels: 44.1 us -> 80.6 us  [fused(): pl.pallas_call(functools.partial(body, dims), out_shape=(jax.ShapeDtypeSt...]
    unnamed x8 -> x3, local copies, waits for them, and re-layouts: 23.9 us -> 0.64 us
    dot_general x2 -> x0, matrix products: 8.67 us -> none  [the longest x1 5.84 us: per_device(): lax.dot_general(lead_all, embed, (((1,), (1,)), ((), ())), preferred_elem...]
    convert_element_type x3 -> x0, other arithmetic: 3.31 us -> none  [the longest x1 1.58 us: per_device(): moe = moe[0].astype(jnp.bfloat16)]
    transpose x0 -> x1, other arithmetic: none -> 2.72 us  [per_device(): return ((scaled[:embed.shape[0]] - norm).T, moe)]
  transfers between devices with their start and end apart: 3 -> 0, of which waited for: 3 -> 0; matrix products, arithmetic and copies ran while one was open for 15% -> 0% of each run, Pallas kernels for 17% -> 0%
where the time goes in v1:
time: 84.8 us; the launch traced here: 84.6 us
  Pallas kernels  80.6 us (95%)
  other arithmetic  2.72 us (3%)
    pallas_call x1, Pallas kernels, fused(): pl.pallas_call(functools.partial(body, dims), out_shape=(jax.ShapeDtypeSt...  80.6 us
    transpose x1, other arithmetic, per_device(): return ((scaled[:embed.shape[0]] - norm).T, moe)  2.72 us

profile of v1, /device:TPU:0, one launch (start us, length us, event | category | flops | bytes accessed | tf_op | source)
XLA Modules:
  0.0 84.6 jit_solution(13745661838416218586)
XLA Ops:
  0.6 80.6 %fused.1 = (f32[1600,256]{1,0:T(8,128)}, f32[1,256]{1,0:T(1,128)}, bf16[64,720]{1,0:T(8,128)(2,1)}) custom-call(bf16[8,2880]{1,0:T(8,128)(2,1)} %lead_ref.1, s32[1,256]{1,0:T(1,128)} %bitcast.14, bf16[1571,2880]{1,0:T(8,128)(2,1)} %embed_ref.1, bf16[8,8,2880]{2,1,0:T(8,128)(2,1)} %bitcast.11, s32[4,64]{1,0:T(4,128)} %bitcast.13, bf16[32,2880]{1,0:T(8,128)(2,1)} %bitcast.12, ...), custom_call_target="tpu_custom_call" | custom-call | tf_op jit(solution)/shard_map/fused/pallas_call | solution.py:574
  81.3 0.0 copy-start
  81.3 2.7 %subtract_bitcast_fusion = f32[256,1571]{0,1:T(8,128)} fusion(f32[1600,256]{1,0:T(8,128)} %get-tuple-element.5, f32[256]{0:T(256)} %bitcast.15), kind=kLoop, calls=%fused_computation | loop fusion | flops 402176 | bytes 3218432 | tf_op jit(solution)/shard_map/transpose | solution.py:604
  84.0 0.0 copy-done
  84.0 0.6 copy.12
Async XLA Ops:
  81.3 2.7 %copy-start = (bf16[64,720]{1,0:T(8,128)(2,1)S(1)}, bf16[64,720]{1,0:T(8,128)(2,1)}, u32[]{:S(2)}) copy-start(bf16[64,720]{1,0:T(8,128)(2,1)} %get-tuple-element.11) | copy-start | bytes 276484

commit v2 on v1

--- a/solution.py
+++ b/solution.py
@@ -58,13 +58,6 @@
     def near(da, d2, d3):
         return wrap(a + da, n1), wrap(p2 + d2, n2), wrap(p3 + d3, n3)
 
-    def others(act_on):
-        for dv in range(nv):
-
-            @pl.loop(0 if dv else 1, ne)
-            def _(de):
-                act_on(wrap(v + dv, nv), wrap(e + de, ne), dv * ne + de)
-
     def slot(g, a_, p2_, p3_, c_):
         v_, e_ = dev(a_, p2_, p3_, c_)
         return v_ * ne + e_ if g == nq else e_ * nv + v_
@@ -107,17 +100,21 @@
 
     barrier = pltpu.get_barrier_semaphore()
 
-    def greet(v_, e_, k):
-        pl.semaphore_signal(barrier, inc=1, device_id=(v_, e_), device_id_type=MESH)
-
-    others(greet)
+    peers = [[dev(*near(d, 0, 0), c) for d in range(1, n1)]]
+    peers += [
+        [
+            dev(*near(0, d2, d3), c if dc == 0 else 1 - c)
+            for dc in range(CORES)
+            for d3 in range(n3)
+            for d2 in range(n2)
+            if dc or d3 or d2
+        ]
+    ]
+    for target in sum(peers, []):
+        pl.semaphore_signal(barrier, inc=1, device_id=target, device_id_type=MESH)
 
     for l in range(min(raw_depth, local)):
         raw[l].start()
-    for l in range(local):
-        wg_in[l].start()
-        wu_in[l].start()
-    embed_in.start()
 
     for copy in small:
         copy.wait()
@@ -145,7 +142,7 @@
 
     held[nq, v * ne + e, :, 0:width] = lead_v[...]
 
-    pl.semaphore_wait(barrier, n - 1)
+    pl.semaphore_wait(barrier, len(sum(peers, [])))
 
     base2 = n1 - 1
     base3 = base2 + (n2 - 1) * n1
@@ -176,7 +173,9 @@
 
     def g_start(g):
         for d in range(1, n1):
-            gcopy(g, slot(g, *near(0, 0, 0), c), d - 1, dev(*near(d, 0, 0), c)).start()
+            gcopy(g, slot(g, a, p2, p3, c), d - 1, dev(*near(d, 0, 0), c)).start()
+
+    def g_own(g):
         forward(g, 0, 0, 0, 1)
 
     def g_one(g):
@@ -254,16 +253,14 @@
             device_id_type=MESH,
         )
 
-    def down_send(q):
-        @pl.loop(0, nx)
-        def _(j):
-            s_send[q, j] = down(j * CORES + 1 - c).astype(s_send.dtype)
-            scopy(q, j).start()
-
-    def down_own(q):
-        @pl.loop(0, nx)
-        def _(j):
-            s_own[q, j] = down(j * CORES + c).astype(s_own.dtype)
+    def down_send(q, dx):
+        j = wrap(x + dx, nx)
+        s_send[q, j] = down(j * CORES + 1 - c).astype(s_send.dtype)
+        scopy(q, j).start()
+
+    def down_own(q, dx):
+        j = wrap(x + dx, nx)
+        s_own[q, j] = down(j * CORES + c).astype(s_own.dtype)
 
     def chip(q, a_, p2_, p3_):
         v_, e_ = dev(a_, p2_, p3_, c)
@@ -303,25 +300,47 @@
             device_id_type=MESH,
         )
 
-    def c_send(q):
-        @pl.loop(0, nx)
-        def _(j):
-            scopy(q, j).wait_recv()
-            if shared:
-                scopy(q, j).wait_send()
-
-        for d3 in range(1, n3):
-
+    def c_unit(q, da, d2, d3):
+        a_, p2_, p3_ = near(da, d2, d3)
+        k = a_ * n2 + p2_
+        sb3[q, d3 - 1, k] = chip(q, a_, p2_, p3_).astype(BF16)
+        c3(q, d3, k, dev(*near(0, 0, d3), c)).start()
+
+    def c_send(q, dx):
+        def lead_x():
             for d2 in range(n2 - 1, -1, -1):
-
-                @pl.loop(0, n1)
-                def _(i):
-                    a_, p2_, p3_ = near(wrap(i + 1, n1), d2, d3)
-                    k = a_ * n2 + p2_
-                    sb3[q, d3 - 1, k] = chip(q, a_, p2_, p3_).astype(BF16)
-                    c3(q, d3, k, dev(*near(0, 0, d3), c)).start()
-
-    def c_three(q):
+                pl.loop(0, n1)(lambda i: c_unit(q, wrap(i + 1, n1), d2, dx))
+
+        def lead_b():
+            for d3 in range(1, n3):
+                pl.loop(0, n1)(lambda i: c_unit(q, wrap(i + 1, n1), dx, d3))
+
+        scopy(q, wrap(x + dx, nx)).wait_recv()
+        if nx == nb:
+            if dx:
+                pl.when(c == 0)(lead_x)
+            pl.when(c == 1)(lead_b)
+        elif dx:
+            lead_x()
+
+    def down_all(q, extra):
+        order = list(range(1, nx)) + [0]
+        for dx in order:
+            down_send(q, dx)
+            if extra:
+                extra.pop(0)()
+        if shared:
+            for dx in order:
+                scopy(q, wrap(x + dx, nx)).wait_send()
+        for dx in order:
+            down_own(q, dx)
+            c_send(q, dx)
+            if extra:
+                extra.pop(0)()
+        for step in extra:
+            step()
+
+    def c_three(q, own):
         def total(da, d2):
             a_, p2_, p3_ = near(da, d2, 0)
             k = a_ * n2 + p2_
@@ -331,7 +350,7 @@
                 part += rb3[q, d3 - 1, k].astype(F32)
             return a_, part
 
-        for d2 in range(n2 - 1, 0, -1):
+        for d2 in range(0 if own else n2 - 1, 0, -1):
 
             @pl.loop(0, n1)
             def _(i):
@@ -339,10 +358,12 @@
                 sb2[q, d2 - 1, a_] = part.astype(BF16)
                 c2(q, d2, a_, dev(*near(0, d2, 0), c)).start()
 
-        @pl.loop(0, n1)
-        def _(i):
-            a_, part = total(wrap(i + 1, n1), 0)
-            acc[q, a_] = part
+        if own:
+
+            @pl.loop(0, n1)
+            def _(i):
+                a_, part = total(wrap(i + 1, n1), 0)
+                acc[q, a_] = part
 
     def c_two(q):
         def total(a_):
@@ -408,101 +429,123 @@
         total = total * jnp.exp(top - peak) + jnp.sum(jnp.exp(part - peak), axis=0, keepdims=True)
         return peak, total
 
-    def stat(v_, e_, s, k):
+    def stat(stage, d):
+        k = sum(len(p) for p in peers[:stage]) + d
         return pltpu.make_async_remote_copy(
-            src_ref=stat_mine,
-            dst_ref=stat_all.at[s],
+            src_ref=stat_mine.at[stage],
+            dst_ref=stat_all.at[k],
             send_sem=st_s.at[k],
-            recv_sem=st_r.at[s],
-            device_id=(v_, e_),
+            recv_sem=st_r.at[k],
+            device_id=peers[stage][d],
             device_id_type=MESH,
         )
 
-    def lm_send(top, total):
-        stat_mine[0:1, :] = top
-        stat_mine[1:2, :] = total
-        stat_all[pl.ds(me, 1)] = stat_mine[...][None]
-        others(lambda v_, e_, k: stat(v_, e_, me, k).start())
-
-    def lm_end():
-        others(lambda v_, e_, k: stat(v_, e_, e_ * nv + v_, k).wait())
-        tops = stat_all[:, 0, :]
-        top = jnp.max(tops, axis=0, keepdims=True)
-        total = jnp.sum(stat_all[:, 1, :] * jnp.exp(tops - top), axis=0, keepdims=True)
-        norm_ref[...] = top + jnp.log(total)
-        for t in range(max(0, tiles - depth), tiles):
-            sc_out(t).wait()
+    def stat_send(stage, top, total):
+        stat_mine[stage, 0:1, :] = top
+        stat_mine[stage, 1:2, :] = total
+        for d in range(len(peers[stage])):
+            stat(stage, d).start()
+
+    def stat_merge(stage):
+        top, total = stat_mine[stage, 0:1, :], stat_mine[stage, 1:2, :]
+        for d in range(len(peers[stage])):
+            stat(stage, d).wait()
+            k = sum(len(p) for p in peers[:stage]) + d
+            peak = jnp.maximum(top, stat_all[k, 0:1, :])
+            total = total * jnp.exp(top - peak) + stat_all[k, 1:2, :] * jnp.exp(
+                stat_all[k, 0:1, :] - peak
+            )
+            top = peak
+        if stage + 1 < len(peers):
+            stat_send(stage + 1, top, total)
+        else:
+            norm_ref[...] = top + jnp.log(total)
 
     last = nq
-    for g in range(groups):
+    g_start(0)
+    g_own(0)
+    for l in range(local - 2):
+        wd_shift(l)
+    for l in range(local):
+        wg_in[l].start()
+        wu_in[l].start()
+    embed_in.start()
+    g_one(0)
+    for g in range(1, nq):
         g_start(g)
-    g_one(0)
-    wd_shift(0)
+    wd_shift(local - 2)
     g_two(0)
-    if nq > 1:
-        g_one(1)
-    wd_shift(1)
+    for g in range(1, nq):
+        g_own(g)
+        g_one(g)
+    g_start(last)
+    wd_shift(local - 1)
     g_three(0)
-    if nq > 1:
-        g_two(1)
-    g_one(last)
+    g_own(last)
     g_sib(0)
     load_x(0)
     load_p(0)
 
     def during(q):
-        steps = []
+        steps = [[] for _ in range(local)]
+        tail = []
+
+        def put(at, *fs):
+            steps[min(at, local - 1)].extend(fs)
+
         if q + 1 < nq:
-            steps += [lambda: g_three(q + 1, [0]), lambda: g_three(q + 1, range(1, n2))]
-            if q + 2 < nq:
-                steps += [lambda: g_one(q + 2), lambda: g_two(q + 2)]
+            put(0, lambda: g_two(q + 1))
+            put(2, lambda: g_three(q + 1, [0]))
+            put(3, lambda: g_three(q + 1, range(1, n2)))
         if q == 0:
-            steps += [lambda: g_two(last)]
-            steps += [lambda: g_three(last, [0]), lambda: g_three(last, range(1, n2))]
+            put(1, lambda: g_one(last))
+            tail += [lambda: None, lambda: g_two(last)]
+        if q == nq - 1:
+            put(1, lambda: g_three(last, [0]))
+            put(local, lambda: g_three(last, range(1, n2)))
         if q:
-            steps += [lambda: c_send(q - 1), lambda: c_three(q - 1)]
-            steps += [lambda: c_two(q - 1), lambda: c_one(q - 1)]
-        return steps
+            put(2, lambda: c_three(q - 1, False))
+            put(local, lambda: c_three(q - 1, True))
+            tail += [lambda: None, lambda: c_two(q - 1)]
+        return steps, tail
 
     for q in range(nq):
         if q:
             g_sib(q)
             load_x(q)
             load_p(q)
-        steps = during(q)
-        work = []
+        steps, tail = during(q)
         for l in range(local):
-            work.append(functools.partial(gate_up, l))
-        work += [lambda: down_send(q), lambda: down_own(q)]
-        for l, step in enumerate(work):
-            if q == 0 and l < local:
+            if q == 0:
                 wg_in[l].wait()
                 wu_in[l].wait()
-                if l >= 2:
-                    wd_shift(l)
-            step()
-            if steps:
-                steps.pop(0)()
-        for step in steps:
-            step()
+            gate_up(l)
+            for extra in steps[l]:
+                extra()
+        down_all(q, tail)
     q = nq - 1
     g_sib(last)
     load_x(last)
-    steps = [lambda: c_send(q), lambda: c_three(q), lambda: c_two(q)]
+    steps = {tiles // 2: lambda: c_three(q, False)}
     top, total = jnp.full((1, n * UNIT), -jnp.inf, F32), jnp.zeros((1, n * UNIT), F32)
     for t in range(tiles):
-        if steps:
-            steps.pop(0)()
+        if t in steps:
+            steps[t]()
         top, total = lm_tile(t, top, total)
-    lm_send(top, total)
-    for step in steps:
-        step()
-    c_one(q)
-    lm_end()
+    stat_send(0, top, total)
+    c_three(q, True)
+    c_two(q)
+    for k in range(q):
+        c_one(k)
     for g in range(groups):
         g_end(g)
-    for q in range(nq):
-        c_end(q)
+    stat_merge(0)
+    c_one(q)
+    for k in range(nq):
+        c_end(k)
+    stat_merge(1)
+    for t in range(max(0, tiles - depth), tiles):
+        sc_out(t).wait()
 
 
 def fused(dims, lead, heat, embed, tok, choice, router, wg, wu, wd):
@@ -521,9 +564,10 @@
     side = -(-max(2 * nexp, rows) // 128) * 128
     n1, n2, n3 = na, nb, nx
     roomy = 3 * nx * nq * tokens * (-(-span // 128) * 128) * 4 < 10 << 20
-    tile = -(-vocab // (64 if roomy else 128)) * 16
+    tile = -(-vocab // (32 if roomy else 128)) * 16
     tiles = -(-vocab // tile)
     link, depth = (F32, tiles) if roomy else (BF16, 2)
+    n_peers = n1 - 1 + n2 * n3 * CORES - 1
     dma = pltpu.SemaphoreType.DMA
     scratch = [
         pltpu.VMEM((vocab, width), BF16),
@@ -552,8 +596,8 @@
         pltpu.VMEM((nq, n1 - 1, per, span), BF16),
         pltpu.VMEM((nq, n1 - 1, per, span), BF16),
         pltpu.VMEM((nq, n1, per, span), F32),
-        pltpu.VMEM((2, tokens), F32),
-        pltpu.VMEM((n, 2, tokens), F32),
+        pltpu.VMEM((2, 2, tokens), F32),
+        pltpu.VMEM((n_peers, 2, tokens), F32),
         dma((6,)),
         dma((tiles,)),
         dma((2, local)),
@@ -568,8 +612,8 @@
         dma((nq, n2 - 1, n1)),
         dma((nq, n1 - 1)),
         dma((nq, n1 - 1)),
-        dma((n,)),
-        dma((n,)),
+        dma((n_peers,)),
+        dma((n_peers,)),
     ]
     return pl.pallas_call(
         functools.partial(body, dims),

time: 84.8 us -> 63.9 us (0.75)
  Pallas kernels: 80.6 us -> 59.7 us
    pallas_call x1, Pallas kernels: 80.6 us -> 59.7 us  [fused(): pl.pallas_call(functools.partial(body, dims), out_shape=(jax.ShapeDtypeSt...]
where the time goes in v2:
time: 63.9 us; the launch traced here: 63.7 us
  Pallas kernels  59.7 us (93%)
  other arithmetic  2.72 us (4%)
  between operations  0.65 us (1%)
  local copies, waits for them, and re-layouts  0.64 us (1%)
    pallas_call x1, Pallas kernels, fused(): pl.pallas_call(functools.partial(body, dims), out_shape=(jax.ShapeDtypeSt...  59.7 us
    transpose x1, other arithmetic, per_device(): return ((scaled[:embed.shape[0]] - norm).T, moe)  2.72 us

profile of v2, /device:TPU:0, one launch (start us, length us, event | category | flops | bytes accessed | tf_op | source)
XLA Modules:
  0.0 63.7 jit_solution(2675092343211568597)
XLA Ops:
  0.6 59.7 %fused.1 = (f32[1600,256]{1,0:T(8,128)}, f32[1,256]{1,0:T(1,128)}, bf16[64,720]{1,0:T(8,128)(2,1)}) custom-call(bf16[8,2880]{1,0:T(8,128)(2,1)} %lead_ref.1, s32[1,256]{1,0:T(1,128)} %bitcast.14, bf16[1571,2880]{1,0:T(8,128)(2,1)} %embed_ref.1, bf16[8,8,2880]{2,1,0:T(8,128)(2,1)} %bitcast.11, s32[4,64]{1,0:T(4,128)} %bitcast.13, bf16[32,2880]{1,0:T(8,128)(2,1)} %bitcast.12, ...), custom_call_target="tpu_custom_call" | custom-call | tf_op jit(solution)/shard_map/fused/pallas_call | solution.py:618
  60.4 0.0 copy-start
  60.4 2.7 %subtract_bitcast_fusion = f32[256,1571]{0,1:T(8,128)} fusion(f32[1600,256]{1,0:T(8,128)} %get-tuple-element.5, f32[256]{0:T(256)} %bitcast.15), kind=kLoop, calls=%fused_computation | loop fusion | flops 402176 | bytes 3218432 | tf_op jit(solution)/shard_map/transpose | solution.py:648
  63.1 0.0 copy-done
  63.1 0.6 %copy.12 = bf16[64,720]{1,0:T(8,128)(2,1)} copy(bf16[64,720]{1,0:T(8,128)(2,1)S(1)} %copy-done) | data formatting | bytes 184320
Async XLA Ops:
  60.4 2.7 %copy-start = (bf16[64,720]{1,0:T(8,128)(2,1)S(1)}, bf16[64,720]{1,0:T(8,128)(2,1)}, u32[]{:S(2)}) copy-start(bf16[64,720]{1,0:T(8,128)(2,1)} %get-tuple-element.11) | copy-start | bytes 276484

commit v3 on v2

--- a/solution.py
+++ b/solution.py
@@ -82,6 +82,8 @@
     wu_in = [pltpu.make_async_copy(wu_ref.at[l], wu_v.at[l], sem_w.at[1, l]) for l in range(local)]
     depth, tile = logits.shape[0], logits.shape[1]
     vocab = embed_ref.shape[0]
+    streamed = tile < vocab
+    tile = tile if streamed else vocab
     tiles = -(-vocab // tile)
 
     def extent(t):
@@ -158,6 +160,12 @@
             device_id_type=MESH,
         )
 
+    def far(i):
+        return jnp.where(2 * a < n1, n1 - i, i)
+
+    def close(i):
+        return jnp.where(i == 0, 0, jnp.where(2 * a < n1, i, n1 - i))
+
     def forward(g, da, d2, d3, stage):
         s = slot(g, *near(da, d2, d3), c)
         if stage <= 1:
@@ -172,7 +180,8 @@
         gcopy(g, s, 0, dev(a, p2, p3, 1 - c)).wait_recv()
 
     def g_start(g):
-        for d in range(1, n1):
+        for i in range(1, n1):
+            d = far(i)
             gcopy(g, slot(g, a, p2, p3, c), d - 1, dev(*near(d, 0, 0), c)).start()
 
     def g_own(g):
@@ -180,7 +189,8 @@
 
     def g_one(g):
         @pl.loop(1, n1)
-        def _(da):
+        def _(i):
+            da = close(i)
             arrive(g, slot(g, *near(da, 0, 0), c))
             forward(g, da, 0, 0, 1)
 
@@ -188,7 +198,8 @@
         for d2 in range(1, n2):
 
             @pl.loop(0, n1)
-            def _(da):
+            def _(i):
+                da = close(i)
                 arrive(g, slot(g, *near(da, d2, 0), c))
                 forward(g, da, d2, 0, 2)
 
@@ -197,7 +208,8 @@
             for d3 in range(1, n3):
 
                 @pl.loop(0, n1)
-                def _(da):
+                def _(i):
+                    da = close(i)
                     arrive(g, slot(g, *near(da, d2, d3), c))
                     forward(g, da, d2, d3, 3)
 
@@ -374,7 +386,8 @@
             return part
 
         @pl.loop(1, n1)
-        def _(da):
+        def _(i):
+            da = far(i)
             a_, p2_, p3_ = near(da, 0, 0)
             sbz[q, da - 1] = total(a_).astype(BF16)
             c1(q, da, dev(a_, p2_, p3_, c)).start()
@@ -421,10 +434,13 @@
             embed_in.wait()
         scale = 1.0 / (0.5 + 0.25 * heat_v[...].astype(F32))
         part = dot_nt(embed_v[at : at + size], x2[...]) * scale
-        if t >= depth:
-            sc_out(t - depth).wait()
-        logits[t % depth, 0:size] = part
-        sc_out(t).start()
+        if streamed:
+            if t >= depth:
+                sc_out(t - depth).wait()
+            logits[t % depth, 0:size] = part
+            sc_out(t).start()
+        else:
+            sc_ref[at : at + size] = part
         peak = jnp.maximum(top, jnp.max(part, axis=0, keepdims=True))
         total = total * jnp.exp(top - peak) + jnp.sum(jnp.exp(part - peak), axis=0, keepdims=True)
         return peak, total
@@ -506,7 +522,7 @@
         if q:
             put(2, lambda: c_three(q - 1, False))
             put(local, lambda: c_three(q - 1, True))
-            tail += [lambda: None, lambda: c_two(q - 1)]
+            tail += [lambda: None, lambda: None, lambda: None, lambda: c_two(q - 1)]
         return steps, tail
 
     for q in range(nq):
@@ -526,13 +542,11 @@
     q = nq - 1
     g_sib(last)
     load_x(last)
-    steps = {tiles // 2: lambda: c_three(q, False)}
     top, total = jnp.full((1, n * UNIT), -jnp.inf, F32), jnp.zeros((1, n * UNIT), F32)
     for t in range(tiles):
-        if t in steps:
-            steps[t]()
         top, total = lm_tile(t, top, total)
     stat_send(0, top, total)
+    c_three(q, False)
     c_three(q, True)
     c_two(q)
     for k in range(q):
@@ -544,7 +558,7 @@
     for k in range(nq):
         c_end(k)
     stat_merge(1)
-    for t in range(max(0, tiles - depth), tiles):
+    for t in range(max(0, tiles - depth) if streamed else tiles, tiles):
         sc_out(t).wait()
 
 
@@ -564,11 +578,13 @@
     side = -(-max(2 * nexp, rows) // 128) * 128
     n1, n2, n3 = na, nb, nx
     roomy = 3 * nx * nq * tokens * (-(-span // 128) * 128) * 4 < 10 << 20
-    tile = -(-vocab // (32 if roomy else 128)) * 16
+    tile = -(-vocab // (16 if roomy else 128)) * 16
     tiles = -(-vocab // tile)
     link, depth = (F32, tiles) if roomy else (BF16, 2)
     n_peers = n1 - 1 + n2 * n3 * CORES - 1
     dma = pltpu.SemaphoreType.DMA
+    shape = jax.ShapeDtypeStruct if tiles > 1 else pltpu.VMEM
+    kept = 0 if tiles > 1 else 2 << 20
     scratch = [
         pltpu.VMEM((vocab, width), BF16),
         pltpu.VMEM((local, ff, width), BF16),
@@ -585,7 +601,7 @@
         pltpu.VMEM((tokens, width), BF16),
         pltpu.VMEM((tokens, 128), F32),
         pltpu.VMEM((local, tokens, ff), BF16),
-        pltpu.VMEM((depth, tile, tokens), F32),
+        pltpu.VMEM((depth, tile, tokens if tiles > 1 else 128), F32),
         pltpu.VMEM((nq, nx, ne, per, span), link),
         pltpu.VMEM((nq, nx, ne, per, span), link),
         pltpu.VMEM((nq, nx, ne, per, span), link),
@@ -618,15 +634,15 @@
     return pl.pallas_call(
         functools.partial(body, dims),
         out_shape=(
-            jax.ShapeDtypeStruct((tiles * tile, tokens), F32),
-            jax.ShapeDtypeStruct((1, tokens), F32),
-            jax.ShapeDtypeStruct((rows, span), BF16),
+            shape((tiles * tile, tokens), F32),
+            shape((1, tokens), F32),
+            shape((rows, span), BF16),
         ),
         in_specs=[ANY] * 9,
-        out_specs=(ANY, VMEM, VMEM),
+        out_specs=(ANY if tiles > 1 else VMEM, VMEM, VMEM),
         scratch_shapes=scratch,
         compiler_params=pltpu.CompilerParams(
-            collective_id=0, has_side_effects=True, vmem_limit_bytes=67043328
+            collective_id=0, has_side_effects=True, vmem_limit_bytes=67043328 - kept
         ),
         name="fused",
     )(lead, heat, embed, tok, choice, router, wg, wu, wd)

time: 63.9 us -> 59.8 us (0.936)
  Pallas kernels: 59.7 us -> 57.1 us
  other arithmetic: 2.72 us -> 1.26 us
    pallas_call x1, Pallas kernels: 59.7 us -> 57.1 us  [fused(): pl.pallas_call(functools.partial(body, dims), out_shape=(shape((tiles * t...]
    transpose x1, other arithmetic: 2.72 us -> 1.26 us  [per_device(): return ((scaled[:embed.shape[0]] - norm).T, moe)]
where the time goes in v3:
time: 59.8 us; the launch traced here: 59.6 us
  Pallas kernels  57.1 us (95%)
  other arithmetic  1.26 us (2%)
  local copies, waits for them, and re-layouts  0.64 us (1%)
  between operations  0.64 us (1%)
    pallas_call x1, Pallas kernels, fused(): pl.pallas_call(functools.partial(body, dims), out_shape=(shape((tiles * t...  57.1 us
    transpose x1, other arithmetic, per_device(): return ((scaled[:embed.shape[0]] - norm).T, moe)  1.26 us

profile of v3, /device:TPU:0, one launch (start us, length us, event | category | flops | bytes accessed | tf_op | source)
XLA Modules:
  0.0 59.6 jit_solution(3797955536866235844)
XLA Ops:
  0.6 57.1 %fused.1 = (f32[1584,256]{1,0:T(8,128)S(1)}, f32[1,256]{1,0:T(1,128)S(1)}, bf16[64,720]{1,0:T(8,128)(2,1)S(1)}) custom-call(bf16[8,2880]{1,0:T(8,128)(2,1)} %lead_ref.1, s32[1,256]{1,0:T(1,128)} %bitcast.15, bf16[1571,2880]{1,0:T(8,128)(2,1)} %embed_ref.1, bf16[8,8,2880]{2,1,0:T(8,128)(2,1)} %bitcast.12, s32[4,64]{1,0:T(4,128)} %bitcast.14, ...), custom_call_target="tpu_custom_call" | custom-call | tf_op jit(solution)/shard_map/fused/pallas_call | solution.py:634
  57.7 1.3 %subtract_bitcast_fusion = f32[256,1571]{0,1:T(8,128)} fusion(f32[1584,256]{1,0:T(8,128)S(1)} %get-tuple-element.5, f32[256]{0:T(256)S(1)} %bitcast.9), kind=kLoop, calls=%fused_computation | loop fusion | flops 402176 | bytes 3218432 | tf_op jit(solution)/shard_map/transpose | solution.py:664
  59.0 0.6 %copy.12 = bf16[64,720]{1,0:T(8,128)(2,1)} copy(bf16[64,720]{1,0:T(8,128)(2,1)S(1)} %get-tuple-element.9) | data formatting | bytes 184320
